TPU v7x, 32 devices: a whole 2x2x4 slice. The times are simulated.
32 devices in a mesh: blk: 8 (over y, x, core), grp: 4 (over z).
Axes of the slice: x: 2, y: 2, z: 4, core: 2. Of those that a mesh axis runs over, the one named last changes fastest.
Arguments:
- samples: float32 [32, 128, 256], P('blk', 'grp'), may hold values from -11 to 11
- pair_table: int32 [32, 16], P('blk'), may hold values from 0 to 31
- assignment: int32 [2, 32], P(None, 'blk'), may hold values from 0 to 127
- band_index: int32 [2], replicated, may hold values from 0 to 1023
Outputs:
- log_weight: float32 [2, 32, 128], P(None, 'blk', 'grp')
All inputs are finite; a program needn't handle non-finite values.
Results may differ from a plain program's by a relative error of at most 0.0003.
Values sent between devices are 32-bit elements; how exact they have to be, the bound alone decides.
No kernel may reach another device: no remote copies, remote signals or barrier semaphores. Data moves between devices by JAX's collectives and lax.ppermute only.
A program may use at most 128 MiB of HBM per device.

v0:
```python
import jax
import jax.numpy as jnp
from jax import lax
from jax.sharding import PartitionSpec as P

PAIRS = 16


def joined_2(shard, axis, combine):
    everything = jax.tree.map(lambda part: lax.all_gather(part, axis), shard)
    initial = jax.tree.map(lambda part: part[0], everything)

    def hop(k, so_far):
        return combine(so_far, jax.tree.map(lambda part: part[k], everything))

    return lax.fori_loop(1, lax.axis_size(axis), hop, initial)


def make_fold(queries, query_norm, band_list, counts):

    def fold(state, shard_rows, offset):
        count_in = shard_rows.shape[0]
        rows_dev = shard_rows.shape[1]

        def compute(inner):
            key_rows = shard_rows.reshape(count_in * rows_dev, shard_rows.shape[2])
            key_norm = jnp.sum(key_rows * key_rows, -1)
            product = jnp.einsum("qd,kd->qk", queries, key_rows, precision=lax.Precision.HIGHEST)
            distance = query_norm[:, None] + key_norm[None, :] - 2.0 * product
            blocks = []
            for band_sq in band_list:
                scores = (-distance / (2.0 * band_sq)).reshape(
                    distance.shape[0], count_in, rows_dev
                )
                peak = jnp.max(scores, -1)
                blocks.append(peak + jnp.log(jnp.sum(jnp.exp(scores - peak[..., None]), -1)))
            update = jnp.stack(blocks)
            return lax.dynamic_update_slice(inner, update, (0, 0, offset))

        needed = jnp.any(counts > 0)
        return lax.cond(needed, compute, lambda inner: inner, state)

    return fold


def per_device(samples, pair_table, assignment, band_index):
    local_subs, rows_dev, width = samples.shape
    rounds = assignment.shape[0]
    group_size = lax.axis_size("grp")
    group_index = lax.axis_index("grp")
    members = local_subs * lax.axis_size("blk")
    band_sq = width * (1.0 + band_index.astype(jnp.float32) / 256.0) / 32.0
    local_pick = assignment - group_index * rows_dev
    onehot = (
        local_pick[:, :, None] == jnp.arange(rows_dev, dtype=jnp.int32)[None, None, :]
    ).astype(jnp.float32)
    picked = jnp.einsum("tsr,srd->td", onehot, samples, precision=lax.Precision.HIGHEST)
    centre = lax.psum(picked, ("blk", "grp")) / members
    member_ids = jnp.arange(members, dtype=jnp.int32)
    count_int = jnp.sum(
        (pair_table[:, :, None] == member_ids[None, None, :]).astype(jnp.int32), axis=1
    )
    counts = count_int.astype(jnp.float32)
    gathered = lax.all_gather(samples, "grp", axis=1, tiled=True)
    query_count = local_subs * rows_dev * group_size
    queries = gathered.reshape(query_count, width)
    query_norm = jnp.sum(queries * queries, -1)
    start_state = jnp.zeros((rounds, query_count, members), jnp.float32)
    fold = make_fold(queries, query_norm, [band_sq[turn] for turn in range(rounds)], count_int)
    partial_value = fold(
        start_state, lax.all_gather(samples, "blk", axis=0, tiled=True), jnp.int32(0)
    )
    split_view = partial_value.reshape(rounds, local_subs, group_size, rows_dev, members)
    swapped = lax.all_to_all(split_view, "grp", split_axis=2, concat_axis=2, tiled=True)
    peak = jnp.max(swapped, 2)
    kernel = peak + jnp.log(jnp.sum(jnp.exp(swapped - peak[:, :, None]), 2))
    weighted = jnp.einsum("tsrm,sm->tsr", kernel, counts, precision=lax.Precision.HIGHEST) / PAIRS
    spread = samples[None] - centre[:, None, None, :]
    logits = weighted - jnp.sum(spread * spread, -1) / (2.0 * band_sq[:, None, None])
    row_peak = jnp.max(logits, -1)
    row_total = jnp.sum(jnp.exp(logits - row_peak[..., None]), -1)

    def combine_pair(first, second):
        joined = jnp.maximum(first[0], second[0])
        return (
            joined,
            first[1] * jnp.exp(first[0] - joined) + second[1] * jnp.exp(second[0] - joined),
        )

    peak_all, total_all = joined_2((row_peak, row_total), "grp", combine_pair)
    return logits - peak_all[..., None] - jnp.log(total_all)[..., None]


def solution(mesh):
    return jax.shard_map(
        per_device,
        mesh=mesh,
        in_specs=(P("blk", "grp", None), P("blk", None), P(None, "blk"), P()),
        out_specs=P(None, "blk", "grp"),
        check_vma=False,
    )
```

profile of v0, /device:TPU:0, one launch (start us, length us, event | category | flops | bytes accessed | tf_op | source)
XLA Modules:
  0.0 123.1 jit_solution(9642932200936565193)
XLA Ops:
  6.5 0.0 all-gather.6.cloned.1.call-start
  6.5 0.7 all-gather.6.cloned.1.call-update
  7.3 0.8 convert_reduce_fusion
  8.0 0.6 compare_reduce_fusion
  9.3 0.7 broadcast_subtract_fusion
  10.0 0.1 copy.19
  10.1 1.2 convolution_bitcast_fusion
  11.3 42.0 %psum.7 = f32[2,256]{1,0:T(2,128)S(1)} all-reduce(f32[2,256]{1,0:T(2,128)S(1)} %convolution_bitcast_fusion), channel_id=1, replica_groups=mesh['blk'=8,'grp'=4] {'blk','grp'}, use_global_device_ids=true, to_apply=%region_12.0 | all-reduce | flops 512 | bytes 4096 | tf_op jit(solution)/shard_map/psum | solution.py:58
  53.2 15.9 %all_gather.18 = f32[4,128,256]{2,1,0:T(8,128)S(1)} all-gather(f32[4,32,256]{2,1,0:T(8,128)} %param.8), channel_id=1, replica_groups=mesh['blk'=8,'grp'=4] {'grp'}, dimensions={1}, use_global_device_ids=true | all-gather | bytes 655360 | tf_op jit(solution)/shard_map/all_gather | solution.py:64
  69.2 0.7 multiply_add_fusion
  69.8 0.0 all-gather.6.cloned.1.call-done
  69.8 14.7 %conditional.1 = (f32[2,512,32]{1,2,0:T(8,128)S(1)}) conditional(s32[]{:T(128)} %convert_element_type.15, () %tuple.36, (f32[4,128,256]{2,1,0:T(8,128)S(1)}, f32[32,32,256]{2,1,0:T(8,128)}, f32[2]{0:T(128)S(1)}) %tuple.37), branch_computations={%region_2.0_spmd, %region_3.10_spmd} | conditional | flops 1617689088 | bytes 25186376 | solution.py:41
  69.8 1.4 %multiply_reduce_fusion = f32[32,32]{1,0:T(8,128)S(1)} fusion(f32[32,32,256]{2,1,0:T(8,128)} %get-tuple-element.164), kind=kLoop, calls=%fused_computation.11 | loop fusion | flops 523264 | bytes 1052672 | tf_op jit(solution)/shard_map/cond/branch_1_fun/reduce_sum | solution.py:27
  71.3 0.1 add.87
  71.3 0.7 fusion.12
  73.4 0.1 multiply_reduce_fusion.1
  73.5 5.3 %broadcast_divide_fusion.1 = (f32[512,1024]{1,0:T(8,128)}, f32[512,1024]{1,0:T(8,128)}) fusion(f32[]{:T(128)} %bitcast.3, f32[]{:T(128)} %bitcast.6, f32[512,256]{1,0:T(8,128)S(1)} %bitcast.71, f32[1024,256]{1,0:T(8,128)} %bitcast.74, f32[1024]{0:T(1024)S(1)} %add.87, f32[512]{0:T(512)S(1)} %bitcast.80), kind=kOutput, calls=%fused_computation.10 | convolution fusion | flops 1613758464 | bytes 5773320 | tf_op jit(solution)/shard_map/cond/branch_1_fun/qd,kd->qk/dot_general | solution.py:28
  78.8 1.9 %copy.16 = f32[512,1024]{0,1:T(8,128)S(1)} copy(f32[512,1024]{1,0:T(8,128)} %get-tuple-element.190) | data formatting | bytes 4194304 | tf_op jit(solution)/shard_map/cond/branch_1_fun/div | solution.py:32
  80.8 0.3 bitcast_reduce_fusion.1
  81.1 0.5 fusion.3
  81.6 1.9 %copy.17 = f32[512,1024]{0,1:T(8,128)S(1)} copy(f32[512,1024]{1,0:T(8,128)} %get-tuple-element.191) | data formatting | bytes 4194304 | tf_op jit(solution)/shard_map/cond/branch_1_fun/div | solution.py:32
  83.6 0.3 bitcast_reduce_fusion
  83.9 0.5 fusion.1
  84.5 0.0 copy-start
  84.5 0.3 reshape.79
  84.8 0.1 copy.28
  84.9 1.0 reshape.97
  85.9 3.8 %all-to-all-start = ((f32[4,1,8192]{2,1,0:T(1,128)}), f32[4,1,8192]{2,1,0:T(1,128)S(1)}, u32[]{:S(2)}, u32[]{:S(2)}) async-start(f32[4,1,8192]{2,1,0:T(1,128)} %reshape.97), calls=%async_computation | async-start | bytes 262144 | tf_op jit(solution)/shard_map/all_to_all | solution.py:74
  89.7 0.0 copy-done
  89.7 0.1 multiply_reduce_fusion.2
  89.8 5.8 %all-to-all-done = f32[4,1,8192]{2,1,0:T(1,128)S(1)} async-done(((f32[4,1,8192]{2,1,0:T(1,128)}), f32[4,1,8192]{2,1,0:T(1,128)S(1)}, u32[]{:S(2)}, u32[]{:S(2)}) %all-to-all-start) | async-done | bytes 131104 | tf_op jit(solution)/shard_map/all_to_all | solution.py:74
  95.6 0.5 broadcast.44
  96.1 1.0 reduce.5
  97.1 0.3 reshape.98
  97.4 0.1 bitcast_reduce_fusion.2
  97.6 0.2 exponential_reduce_fusion
  97.8 0.2 fusion.6
  98.0 0.2 fusion.11
  98.2 0.2 exponential_reduce_fusion.1
  98.3 9.0 %all-gather.3 = f32[4,2,4]{2,1,0:T(2,128)S(1)} all-gather(f32[1,2,4]{2,1,0:T(2,128)S(1)} %bitcast.79), channel_id=3, replica_groups=mesh['blk'=8,'grp'=4] {'grp'}, dimensions={0}, use_global_device_ids=true | all-gather | bytes 160 | tf_op jit(solution)/shard_map/all_gather | solution.py:10
  107.3 8.2 %all-gather.2 = f32[4,2,4]{2,1,0:T(2,128)S(1)} all-gather(f32[1,2,4]{2,1,0:T(2,128)S(1)} %bitcast.77), channel_id=2, replica_groups=mesh['blk'=8,'grp'=4] {'grp'}, dimensions={0}, use_global_device_ids=true | all-gather | bytes 160 | tf_op jit(solution)/shard_map/all_gather | solution.py:10
  115.5 0.1 while.17
  115.6 0.7 subtract_subtract_fusion
  (12 shorter events, 0.2 us)
Async XLA Ops:
  6.5 63.3 %all-gather.6.cloned.1.call-start = ((), (), s32[]{:S(2)}) async-start(), calls=%async_computation.1 | async-start | bytes 1179648 | tf_op jit(solution)/shard_map/all_gather | solution.py:71
  84.5 5.2 %copy-start = (f32[4,32,256]{2,1,0:T(8,128)S(1)}, f32[4,32,256]{2,1,0:T(8,128)}, u32[]{:S(2)}) copy-start(f32[4,32,256]{2,1,0:T(8,128)} %param.8) | copy-start | bytes 393220
  85.9 9.7 %all-to-all-start = ((f32[4,1,8192]{2,1,0:T(1,128)}), f32[4,1,8192]{2,1,0:T(1,128)S(1)}, u32[]{:S(2)}, u32[]{:S(2)}) async-start(f32[4,1,8192]{2,1,0:T(1,128)} %reshape.97), calls=%async_computation | async-start | bytes 262144 | tf_op jit(solution)/shard_map/all_to_all | solution.py:74
Sparse Core Ops, SparseCore 0:
  9.2 26.2 all-gather.5
where the time goes:
time: 124 us; the launch traced here: 123 us
  blocking collectives  75 us (60%)
  between operations  14.1 us (11%)
  other arithmetic  8.66 us (7%)
  local copies, waits for them, and re-layouts  6.86 us (6%)
  matrix products  6.7 us (5%)
  waiting for transfers between devices  6.5 us (5%)
  starting transfers between devices  3.8 us (3%)
  loops' own time  1.43 us (1%)
    psum x1, blocking collectives, per_device(): centre = lax.psum(picked, ('blk', 'grp')) / members  42 us
    all_gather x2, blocking collectives, joined_2(): everything = jax.tree.map(lambda part: lax.all_gather(part, axis), shard)  17.2 us
    all_gather x1, blocking collectives, per_device(): gathered = lax.all_gather(samples, 'grp', axis=1, tiled=True)  15.9 us
    all_to_all x1, waiting for transfers between devices, per_device(): lax.all_to_all(split_view, 'grp', split_axis=2, concat_axis=2, tiled=True)  5.79 us
    dot_general x1, matrix products, compute(): jnp.einsum('qd,kd->qk', queries, key_rows, precision=lax.Precision.HIGHEST)  5.35 us
    div x2, local copies, waits for them, and re-layouts, compute(): -distance / (2.0 * band_sq)  3.84 us
    all_to_all x1, starting transfers between devices, per_device(): lax.all_to_all(split_view, 'grp', split_axis=2, concat_axis=2, tiled=True)  3.8 us
  transfers between devices with their start and end apart: 2, of which 1 were waited for; matrix products, arithmetic and copies ran while one was open for 3% of the time, Pallas kernels for 0%

commit v1 on v0

--- a/solution.py
+++ b/solution.py
@@ -61,7 +61,10 @@
         (pair_table[:, :, None] == member_ids[None, None, :]).astype(jnp.int32), axis=1
     )
     counts = count_int.astype(jnp.float32)
-    gathered = lax.all_gather(samples, "grp", axis=1, tiled=True)
+    size = lax.axis_size("grp")
+    parts = jnp.stack([samples for _ in range(size)])
+    parts = lax.all_to_all(parts, "grp", split_axis=0, concat_axis=0)
+    gathered = jnp.concatenate(parts, axis=1)
     query_count = local_subs * rows_dev * group_size
     queries = gathered.reshape(query_count, width)
     query_norm = jnp.sum(queries * queries, -1)

time: 124 us -> 113 us (0.911)
  blocking collectives: 75 us -> 57.9 us
  starting transfers between devices: 3.8 us -> 9.9 us
  local copies, waits for them, and re-layouts: 6.86 us -> 8.7 us
    all_gather x1 -> x0, blocking collectives: 15.9 us -> none  [per_device(): gathered = lax.all_gather(samples, 'grp', axis=1, tiled=True)]
    all_to_all x0 -> x1, starting transfers between devices: none -> 6.35 us  [per_device(): parts = lax.all_to_all(parts, 'grp', split_axis=0, concat_axis=0)]
    another operation x0 -> x1, local copies, waits for them, and re-layouts: none -> 1.75 us  [per_device(): parts = jnp.stack([samples for _ in range(size)])]
  transfers between devices with their start and end apart: 2 -> 3, of which waited for: 1 -> 1; matrix products, arithmetic and copies ran while one was open for 3% -> 5% of each run, Pallas kernels for 0% -> 0%
where the time goes in v1:
time: 113 us
  blocking collectives  57.9 us (51%)
  between operations  14.1 us (12%)
  starting transfers between devices  9.9 us (9%)
  other arithmetic  8.73 us (8%)
  local copies, waits for them, and re-layouts  8.7 us (8%)
  waiting for transfers between devices  6.5 us (6%)
  matrix products  5.48 us (5%)
  loops' own time  1.46 us (1%)
    psum x1, blocking collectives, per_device(): centre = lax.psum(picked, ('blk', 'grp')) / members  40.8 us
    all_gather x2, blocking collectives, joined_2(): everything = jax.tree.map(lambda part: lax.all_gather(part, axis), shard)  17.2 us
    all_to_all x1, starting transfers between devices, per_device(): parts = lax.all_to_all(parts, 'grp', split_axis=0, concat_axis=0)  6.35 us
    all_to_all x1, waiting for transfers between devices, per_device(): lax.all_to_all(split_view, 'grp', split_axis=2, concat_axis=2, tiled=True)  5.79 us
    dot_general x1, matrix products, compute(): jnp.einsum('qd,kd->qk', queries, key_rows, precision=lax.Precision.HIGHEST)  4.13 us
    div x2, local copies, waits for them, and re-layouts, compute(): -distance / (2.0 * band_sq)  3.84 us
    all_to_all x1, starting transfers between devices, per_device(): lax.all_to_all(split_view, 'grp', split_axis=2, concat_axis=2, tiled=True)  3.55 us
  transfers between devices with their start and end apart: 3, of which 1 were waited for; matrix products, arithmetic and copies ran while one was open for 5% of the time, Pallas kernels for 0%

profile of v1, /device:TPU:0, one launch (start us, length us, event | category | flops | bytes accessed | tf_op | source)
XLA Modules:
  0.0 112.8 jit_solution(1516808820120411792)
XLA Ops:
  6.5 0.0 all-gather.6.cloned.1.call-start
  6.5 0.7 all-gather.6.cloned.1.call-update
  7.3 1.7 %stack.5 = f32[4,4,32,256]{3,2,1,0:T(8,128)} broadcast(f32[4,32,256]{2,1,0:T(8,128)} %param.8), dimensions={1,2,3} | broadcast | bytes 655360 | tf_op jit(solution)/shard_map/stack | solution.py:65
  9.0 6.3 %all-to-all-start = ((f32[4,4,32,256]{3,2,1,0:T(8,128)}), f32[4,4,32,256]{3,2,1,0:T(8,128)S(1)}, u32[]{:S(2)}, u32[]{:S(2)}) async-start(f32[4,4,32,256]{3,2,1,0:T(8,128)} %stack.5), calls=%async_computation | async-start | bytes 1048576 | tf_op jit(solution)/shard_map/all_to_all | solution.py:66
  15.3 0.8 convert_reduce_fusion
  16.1 0.6 compare_reduce_fusion
  17.4 0.7 broadcast_subtract_fusion
  18.1 0.1 copy.22
  18.2 1.2 %convolution_bitcast_fusion = f32[2,256]{1,0:T(2,128)S(1)} fusion(f32[4,32,256]{2,1,0:T(8,128)} %param.8, s32[2,4]{0,1:T(4,128)S(1)} %copy.22), kind=kOutput, calls=%fused_computation.22 | convolution fusion | flops 786688 | bytes 133152 | tf_op jit(solution)/shard_map/tsr,srd->td/dot_general | solution.py:57
  19.4 40.8 %psum.7 = f32[2,256]{1,0:T(2,128)S(1)} all-reduce(f32[2,256]{1,0:T(2,128)S(1)} %convolution_bitcast_fusion), channel_id=1, replica_groups=mesh['blk'=8,'grp'=4] {'blk','grp'}, use_global_device_ids=true, to_apply=%region_12.0 | all-reduce | flops 512 | bytes 4096 | tf_op jit(solution)/shard_map/psum | solution.py:58
  60.1 0.7 multiply_add_fusion
  60.8 0.0 all-to-all-done
  60.8 0.0 all-gather.6.cloned.1.call-done
  60.8 13.6 %conditional.1 = (f32[2,512,32]{1,2,0:T(8,128)S(1)}) conditional(s32[]{:T(128)} %convert_element_type.15, () %tuple.36, (f32[4,4,32,256]{3,2,0,1:T(8,128)S(1)}, f32[32,32,256]{2,1,0:T(8,128)}, f32[2]{0:T(128)S(1)}) %tuple.66), branch_computations={%region_2.0_spmd, %region_3.10_spmd} | conditional | flops 1617689088 | bytes 29909092 | solution.py:41
  60.8 0.0 copy-start.1
  60.8 0.2 multiply_reduce_fusion.1
  61.0 0.1 reduce_sum.68
  61.1 1.5 %multiply_reduce_fusion = f32[32,32]{1,0:T(8,128)S(1)} fusion(f32[32,32,256]{2,1,0:T(8,128)} %get-tuple-element.164), kind=kLoop, calls=%fused_computation.11 | loop fusion | flops 523264 | bytes 1052672 | tf_op jit(solution)/shard_map/cond/branch_1_fun/reduce_sum | solution.py:27
  62.6 0.1 add.87
  62.7 0.7 fusion.12
  64.7 0.0 copy-done.1
  64.7 4.1 %broadcast_divide_fusion.1 = (f32[512,1024]{1,0:T(8,128)}, f32[512,1024]{1,0:T(8,128)}) fusion(f32[]{:T(128)} %bitcast.2, f32[]{:T(128)} %bitcast.5, f32[512,256]{1,0:T(8,128)S(1)} %bitcast.76, f32[1024,256]{1,0:T(8,128)S(1)} %bitcast.74, f32[1024]{0:T(1024)S(1)} %add.87, f32[512]{0:T(512)S(1)} %reduce_sum.68), kind=kOutput, calls=%fused_computation.10 | convolution fusion | flops 1613758464 | bytes 5773320 | tf_op jit(solution)/shard_map/cond/branch_1_fun/qd,kd->qk/dot_general | solution.py:28
  68.8 1.9 %copy.18 = f32[512,1024]{0,1:T(8,128)S(1)} copy(f32[512,1024]{1,0:T(8,128)} %get-tuple-element.199) | data formatting | bytes 4194304 | tf_op jit(solution)/shard_map/cond/branch_1_fun/div | solution.py:32
  70.7 0.3 bitcast_reduce_fusion.1
  71.1 0.5 fusion.3
  71.6 1.9 %copy.19 = f32[512,1024]{0,1:T(8,128)S(1)} copy(f32[512,1024]{1,0:T(8,128)} %get-tuple-element.200) | data formatting | bytes 4194304 | tf_op jit(solution)/shard_map/cond/branch_1_fun/div | solution.py:32
  73.5 0.3 bitcast_reduce_fusion
  73.9 0.5 fusion.1
  74.4 0.0 copy-start
  74.5 0.3 reshape.80
  74.7 0.1 copy.33
  74.9 1.0 reshape.98
  75.9 3.6 %all-to-all-start.1 = ((f32[4,1,8192]{2,1,0:T(1,128)}), f32[4,1,8192]{2,1,0:T(1,128)S(1)}, u32[]{:S(2)}, u32[]{:S(2)}) async-start(f32[4,1,8192]{2,1,0:T(1,128)} %reshape.98), calls=%async_computation.1 | async-start | bytes 262144 | tf_op jit(solution)/shard_map/all_to_all | solution.py:77
  79.4 0.0 copy-done
  79.4 0.1 multiply_reduce_fusion.2
  79.5 5.8 %all-to-all-done.1 = f32[4,1,8192]{2,1,0:T(1,128)S(1)} async-done(((f32[4,1,8192]{2,1,0:T(1,128)}), f32[4,1,8192]{2,1,0:T(1,128)S(1)}, u32[]{:S(2)}, u32[]{:S(2)}) %all-to-all-start.1) | async-done | bytes 131104 | tf_op jit(solution)/shard_map/all_to_all | solution.py:77
  85.3 0.5 broadcast.46
  85.8 1.0 reduce.5
  86.8 0.3 reshape.99
  87.1 0.1 bitcast_reduce_fusion.2
  87.3 0.2 exponential_reduce_fusion
  87.5 0.2 fusion.6
  87.7 0.2 fusion.11
  87.9 0.2 exponential_reduce_fusion.1
  88.0 9.0 %all-gather.3 = f32[4,2,4]{2,1,0:T(2,128)S(1)} all-gather(f32[1,2,4]{2,1,0:T(2,128)S(1)} %bitcast.80), channel_id=3, replica_groups=mesh['blk'=8,'grp'=4] {'grp'}, dimensions={0}, use_global_device_ids=true | all-gather | bytes 160 | tf_op jit(solution)/shard_map/all_gather | solution.py:10
  97.0 8.2 %all-gather.2 = f32[4,2,4]{2,1,0:T(2,128)S(1)} all-gather(f32[1,2,4]{2,1,0:T(2,128)S(1)} %bitcast.78), channel_id=2, replica_groups=mesh['blk'=8,'grp'=4] {'grp'}, dimensions={0}, use_global_device_ids=true | all-gather | bytes 160 | tf_op jit(solution)/shard_map/all_gather | solution.py:10
  105.2 0.1 while.17
  105.3 0.7 subtract_subtract_fusion
  (12 shorter events, 0.2 us)
Async XLA Ops:
  6.5 54.3 %all-gather.6.cloned.1.call-start = ((), (), s32[]{:S(2)}) async-start(), calls=%async_computation.2 | async-start | bytes 1179648 | tf_op jit(solution)/shard_map/all_gather | solution.py:74
  9.0 51.8 %all-to-all-start = ((f32[4,4,32,256]{3,2,1,0:T(8,128)}), f32[4,4,32,256]{3,2,1,0:T(8,128)S(1)}, u32[]{:S(2)}, u32[]{:S(2)}) async-start(f32[4,4,32,256]{3,2,1,0:T(8,128)} %stack.5), calls=%async_computation | async-start | bytes 1048576 | tf_op jit(solution)/shard_map/all_to_all | solution.py:66
  60.8 3.8 %copy-start.1 = (f32[32,32,256]{2,1,0:T(8,128)S(1)}, f32[32,32,256]{2,1,0:T(8,128)}, u32[]{:S(2)}) copy-start(f32[32,32,256]{2,1,0:T(8,128)} %get-tuple-element.164) | copy-start | bytes 3145732 | tf_op jit(solution)/shard_map/cond
  74.4 5.0 %copy-start = (f32[4,32,256]{2,1,0:T(8,128)S(1)}, f32[4,32,256]{2,1,0:T(8,128)}, u32[]{:S(2)}) copy-start(f32[4,32,256]{2,1,0:T(8,128)} %param.8) | copy-start | bytes 393220
  75.9 9.5 %all-to-all-start.1 = ((f32[4,1,8192]{2,1,0:T(1,128)}), f32[4,1,8192]{2,1,0:T(1,128)S(1)}, u32[]{:S(2)}, u32[]{:S(2)}) async-start(f32[4,1,8192]{2,1,0:T(1,128)} %reshape.98), calls=%async_computation.1 | async-start | bytes 262144 | tf_op jit(solution)/shard_map/all_to_all | solution.py:77
Sparse Core Ops, SparseCore 0:
  9.2 26.1 all-gather.5
